TPU v7x, 32 devices: a whole 2x2x4 slice. The times are simulated.
32 devices in a mesh: span: 8 (over z, x), chord: 4 (over y, core).
Axes of the slice: x: 2, y: 2, z: 4, core: 2. Of those that a mesh axis runs over, the one named last changes fastest.
Arguments:
- fluid_state: float32 [4, 256, 128, 128], P(None, 'span', 'chord'), may hold values from -6 to 6
- shell_disp: float32 [3, 1024, 512], P(None, 'span', 'chord'), may hold values from -6 to 6
- shell_vel: float32 [3, 1024, 512], P(None, 'span', 'chord'), may hold values from -6 to 6
- owners: int32 [32768, 4], P(('span', 'chord')), may hold values from 0 to 31, all different within a row; in each aligned block of 1024 rows (0 to 1023, 1024 to 2047, ...) at most 256 rows name the same one
- node_local: int32 [32768, 4], P(('span', 'chord')), may hold values from 0 to 16383
- rbf_weight: float32 [32768, 4], P(('span', 'chord')), may hold values from 0.2 to 1
- normals: float32 [3, 32768], P(None, ('span', 'chord')), may hold values from -6 to 6
Outputs:
- fluid_next: float32 [4, 256, 128, 128], P(None, 'span', 'chord')
- interface_motion: float32 [6, 32768], P(None, ('span', 'chord'))
- disp_next: float32 [3, 1024, 512], P(None, 'span', 'chord')
- vel_next: float32 [3, 1024, 512], P(None, 'span', 'chord')
Inputs may be any that keep to these rules, and one draw needn't show every extreme that they name: Each interface point names 4 different owners; the points of one device name no owner more than 256 times, a bound that some block reaches.
All inputs are finite; a program needn't handle non-finite values.
Results may differ from a plain program's by a relative error of at most 0.00007.
Values sent between devices are 32-bit elements; how exact they have to be, the bound alone decides.
No kernel may reach another device: no remote copies, remote signals or barrier semaphores. Data moves between devices by JAX's collectives and lax.ppermute only.
A program may use at most 64 MiB of HBM per device.

v0:
```python
import jax
import jax.numpy as jnp
from jax import lax
from jax.sharding import PartitionSpec as P

flow_speed = 0.5
time_step = 0.4
stiffness = 0.5
damping = 0.2
shell_step = 0.3


def with_halo(value, sides, width):
    for axis, dim in sides:
        size, length = (lax.axis_size(axis), value.shape[dim])
        up = [(i, (i + 1) % size) for i in range(size - 1)]
        down = [(j, i) for i, j in up]
        last = lax.slice_in_dim(value, length - width, length, axis=dim)
        leading = lax.slice_in_dim(value, 0, width, axis=dim)
        before = lax.ppermute(last, axis, up)
        after = lax.ppermute(leading, axis, down)
        value = jnp.concatenate([before, value, after], axis=dim)
    return value


def central(padded, direction):
    length = padded.shape[direction] - 6

    def window(offset):
        return lax.slice_in_dim(padded, 3 + offset, 3 + offset + length, axis=direction)

    return (
        45.0 * (window(1) - window(-1)) - 9.0 * (window(2) - window(-2)) + (window(3) - window(-3))
    ) / 60.0


def stencil_coef(distance):
    size = jnp.abs(distance)
    value = jnp.where(size == 1, 45.0, jnp.where(size == 2, -9.0, jnp.where(size == 3, 1.0, 0.0)))
    return value * jnp.sign(distance).astype(jnp.float32) / 60.0


def normal_tables(length):
    source = lax.broadcasted_iota(jnp.int32, (length, length), 0)
    target = lax.broadcasted_iota(jnp.int32, (length, length), 1)
    inner = stencil_coef(source - target)
    ghost = jnp.where(source < 3, stencil_coef(-(source + 1 + target)), 0.0)
    pressure_table = inner + ghost
    normal_table = inner - ghost
    wall_row = 2.0 * jnp.sum(ghost, axis=0)
    return (pressure_table, normal_table, wall_row)


def normal_derivatives(fluid, wall_motion):
    cells_x, cells_y, length = (fluid.shape[1], fluid.shape[2], fluid.shape[3])
    pressure_table, normal_table, wall_row = normal_tables(length)
    pressure_flat = fluid[0].reshape(cells_x * cells_y, length)
    normal_flat = fluid[3].reshape(cells_x * cells_y, length)
    dz_pressure = jnp.dot(
        pressure_flat,
        pressure_table,
        precision=lax.Precision.HIGHEST,
        preferred_element_type=jnp.float32,
    )
    dz_normal = jnp.dot(
        normal_flat,
        normal_table,
        precision=lax.Precision.HIGHEST,
        preferred_element_type=jnp.float32,
    )
    dz_normal = dz_normal + wall_motion[2].reshape(-1)[:, None] * wall_row[None, :]
    return (
        dz_pressure.reshape(cells_x, cells_y, length),
        dz_normal.reshape(cells_x, cells_y, length),
    )


def fluid_rates(span_padded, chord_padded, dz_pressure, dz_normal):
    along_span = central(span_padded, 1)
    along_chord = central(chord_padded, 2)
    rate_p = -flow_speed * along_span[0] - (along_span[1] + along_chord[1] + dz_normal)
    rate_u = -flow_speed * along_span[1] - along_span[0]
    rate_v = -flow_speed * along_span[2] - along_chord[0]
    rate_w = -flow_speed * along_span[3] - dz_pressure
    return jnp.stack([rate_p, rate_u, rate_v, rate_w])


def laplacian(padded):
    center = padded[:, 1:-1, 1:-1]
    return (
        padded[:, 2:, 1:-1]
        + padded[:, :-2, 1:-1]
        + padded[:, 1:-1, 2:]
        + padded[:, 1:-1, :-2]
        - 4.0 * center
    )


def body(fluid_state, shell_disp, shell_vel, owners, node_local, rbf_weight, normals):
    span_count = lax.axis_size("span")
    chord_count = lax.axis_size("chord")
    devices = span_count * chord_count
    points, stencil = owners.shape
    capacity = max(2, (2 * points * stencil + devices - 1) // devices)
    owner_ids = owners.reshape(-1)
    node_ids = node_local.reshape(-1)
    columns = jnp.arange(devices, dtype=jnp.int32)
    onehot = (owner_ids[:, None] == columns[None, :]).astype(jnp.int32)
    before = jnp.cumsum(onehot, axis=0) - onehot
    order_in = jnp.sum(before * onehot, axis=1)
    slot_index = owner_ids * capacity + order_in
    requests = jnp.zeros((devices * capacity,), jnp.int32).at[slot_index].set(node_ids)
    asked_nodes = lax.all_to_all(
        requests, ("span", "chord"), split_axis=0, concat_axis=0, tiled=True
    )
    rows_x, rows_y = (shell_disp.shape[1], shell_disp.shape[2])
    stacked = jnp.concatenate([shell_disp, shell_vel], axis=0).reshape(6, rows_x * rows_y)
    picked = jnp.take(stacked, asked_nodes, axis=1)
    replies = lax.all_to_all(picked, ("span", "chord"), split_axis=1, concat_axis=1, tiled=True)
    motion = jnp.take(replies, slot_index, axis=1).reshape(6, points, stencil)
    interface_motion = jnp.sum(motion * rbf_weight[None], axis=2)
    cells_x, cells_y = (fluid_state.shape[1], fluid_state.shape[2])
    wall_motion = interface_motion[3:].reshape(3, cells_x, cells_y)
    padded_all = with_halo(fluid_state, (("span", 1), ("chord", 2)), 3)
    span_padded = padded_all[:, :, 3:-3]
    chord_padded = padded_all[0::2, 3:-3]
    dz_pressure, dz_normal = normal_derivatives(fluid_state, wall_motion)
    fluid_next = fluid_state + time_step * fluid_rates(
        span_padded, chord_padded, dz_pressure, dz_normal
    )
    pressure = fluid_next[0, :, :, 0].reshape(-1)
    surface_load = normals * pressure[None]
    contrib = (surface_load[:, :, None] * rbf_weight[None]).reshape(3, -1)
    outgoing = jnp.zeros((3, devices * capacity), jnp.float32).at[:, slot_index].set(contrib)
    arrived = lax.all_to_all(outgoing, ("span", "chord"), split_axis=1, concat_axis=1, tiled=True)
    shell_force = (
        jnp.zeros((3, rows_x * rows_y), jnp.float32)
        .at[:, asked_nodes]
        .add(arrived)
        .reshape(3, rows_x, rows_y)
    )
    shell_padded = with_halo(shell_disp, (("span", 1), ("chord", 2)), 1)
    bending = laplacian(shell_padded)
    acceleration = stiffness * bending + shell_force - damping * shell_vel
    vel_next = shell_vel + shell_step * acceleration
    disp_next = shell_disp + shell_step * vel_next
    return (fluid_next, interface_motion, disp_next, vel_next)


def solution(mesh):
    placed = (
        P(None, "span", "chord", None),
        P(None, "span", "chord"),
        P(None, "span", "chord"),
        P(("span", "chord"), None),
        P(("span", "chord"), None),
        P(("span", "chord"), None),
        P(None, ("span", "chord")),
    )
    return jax.shard_map(
        body,
        mesh=mesh,
        in_specs=placed,
        out_specs=(
            P(None, "span", "chord", None),
            P(None, ("span", "chord")),
            P(None, "span", "chord"),
            P(None, "span", "chord"),
        ),
        check_vma=False,
    )
```

profile of v0, /device:TPU:8, one launch (start us, length us, event | category | flops | bytes accessed | tf_op | source)
XLA Modules:
  0.0 256.4 jit_solution(6483146441333637341)
XLA Ops:
  3.5 9.2 %reduce-window.6 = s32[32,32,128]{2,1,0:T(8,128)S(1)} reduce-window(s32[32,32,128]{2,1,0:T(8,128)S(1)} %fusion.25, s32[]{:T(128)} %constant.34.clone.1), window={size=1x1x128 pad=0_0x0_0x127_0}, to_apply=%region_0.0 | reduce-window | flops 16646144 | bytes 1048580 | tf_op jit(solution)/shard_map/reduce-window
  14.9 16.1 %scatter_custom_fusion = s32[8192]{0:T(1024)} fusion(s32[4096]{0:T(1024)S(1)} %bitcast.73, s32[4096]{0:T(1024)S(1)} %reshape.173, s32[]{:T(128)} %constant.34.clone.1), kind=kCustom, calls=%fused_computation.117 | custom fusion | bytes 32772 | tf_op jit(solution)/shard_map/scatter | solution.py:112
  31.0 6.1 %all-to-all-start = ((s32[32,256,1]{1,2,0:T(1,128)}), s32[32,256,1]{1,2,0:T(1,128)}, u32[]{:S(2)}, u32[]{:S(2)}) async-start(s32[32,256,1]{1,2,0:T(1,128)} %bitcast.5), calls=%async_computation | async-start | bytes 65536 | tf_op jit(solution)/shard_map/all_to_all | solution.py:113
  37.9 3.5 %collective-permute-start.1 = (f32[4,3,32,128]{3,2,1,0:T(8,128)}, f32[4,3,32,128]{3,2,1,0:T(8,128)}, u32[]{:S(2)}, u32[]{:S(2)}) collective-permute-start(f32[4,3,32,128]{3,2,1,0:T(8,128)} %get-tuple-element.34), channel_id=1, source_target_pairs={{0,4},{4,8},{8,12},{12,16},{16,20},{20,24},{24,28},{1,5},{5,9},{9,... | collective-permute-start | bytes 589832 | tf_op jit(solution)/shard_map/ppermute | solution.py:20
  41.4 3.4 %collective-permute-start = (f32[4,3,32,128]{3,2,1,0:T(8,128)}, f32[4,3,32,128]{3,2,1,0:T(8,128)}, u32[]{:S(2)}, u32[]{:S(2)}) collective-permute-start(f32[4,3,32,128]{3,2,1,0:T(8,128)} %get-tuple-element.33), channel_id=1, source_target_pairs={{4,0},{8,4},{12,8},{16,12},{20,16},{24,20},{28,24},{5,1},{9,5},{13... | collective-permute-start | bytes 589832 | tf_op jit(solution)/shard_map/ppermute | solution.py:21
  45.3 3.1 %collective-permute-start.4 = (f32[3,1,128]{2,1,0:T(1,128)}, f32[3,1,128]{2,1,0:T(1,128)S(1)}, u32[]{:S(2)}, u32[]{:S(2)}) collective-permute-start(f32[3,1,128]{2,1,0:T(1,128)} %get-tuple-element.38), channel_id=1, source_target_pairs={{4,0},{8,4},{12,8},{16,12},{20,16},{24,20},{28,24},{5,1},{9,5},{13... | collective-permute-start | bytes 4616 | tf_op jit(solution)/shard_map/ppermute | solution.py:21
  48.4 2.7 %collective-permute-start.5 = (f32[3,1,128]{2,1,0:T(1,128)}, f32[3,1,128]{2,1,0:T(1,128)}, u32[]{:S(2)}, u32[]{:S(2)}) collective-permute-start(f32[3,1,128]{2,1,0:T(1,128)} %get-tuple-element.37), channel_id=1, source_target_pairs={{0,4},{4,8},{8,12},{12,16},{16,20},{20,24},{24,28},{1,5},{5,9},{9,... | collective-permute-start | bytes 4616 | tf_op jit(solution)/shard_map/ppermute | solution.py:20
  57.0 4.7 %copy.82 = f32[6,128,128]{0,2,1:T(8,128)} copy(f32[6,128,128]{2,1,0:T(8,128)S(1)} %pad_maximum_fusion.1) | data formatting | bytes 786432 | tf_op jit(solution)/shard_map/concatenate | solution.py:117
  66.2 31.2 %gather_fusion = f32[8192,6]{1,0:T(8,128)} fusion(f32[6,16384]{0,1:T(8,128)} %bitcast.58, s32[8192]{0:T(1024)S(1)} %broadcast_clamp_fusion), kind=kCustom, calls=%fused_computation | custom fusion | bytes 425984 | tf_op jit(solution)/shard_map/jit(_take)/gather | solution.py:118
  97.5 2.8 %copy.83 = f32[6,32,256]{2,0,1:T(8,128)S(1)} copy(f32[6,32,256]{0,2,1:T(8,128)} %bitcast.61) | data formatting | bytes 393216 | tf_op jit(solution)/shard_map/jit(_take)/gather | solution.py:118
  101.9 4.9 %all-to-all-start.1 = ((f32[6,32,256]{2,0,1:T(8,128)}), f32[6,32,256]{2,0,1:T(8,128)S(1)}, u32[]{:S(2)}, u32[]{:S(2)}) async-start(f32[6,32,256]{2,0,1:T(8,128)} %broadcast_select_fusion), calls=%async_computation.1 | async-start | bytes 524288 | tf_op jit(solution)/shard_map/all_to_all | solution.py:119
  109.7 1.3 collective-permute-start.3
  111.0 3.2 %collective-permute-start.2 = (f32[4,38,3,128]{3,2,1,0:T(4,128)S(1)}, f32[4,38,3,128]{3,2,1,0:T(4,128)S(1)}, u32[]{:S(2)}, u32[]{:S(2)}) collective-permute-start(f32[4,38,3,128]{3,2,1,0:T(4,128)S(1)} %get-tuple-element.24), channel_id=1, source_target_pairs={{0,1},{1,2},{2,3},{4,5},{5,6},{6,7},{8,9},{9,10},{10,11},{12,13},{... | collective-permute-start | bytes 700424 | tf_op jit(solution)/shard_map/ppermute | solution.py:20
  114.3 1.9 fusion.3
  116.7 1.6 fusion.14
  118.3 2.6 %copy.84 = f32[6,32,256]{0,2,1:T(8,128)} copy(f32[6,32,256]{2,0,1:T(8,128)S(1)} %all-to-all-done.1) | data formatting | bytes 393216 | tf_op jit(solution)/shard_map/all_to_all | solution.py:119
  121.0 16.4 %gather_fusion.1 = f32[4096,6]{1,0:T(8,128)} fusion(f32[6,8192]{0,1:T(8,128)} %bitcast.60, s32[4096]{0:T(1024)S(1)} %copy-done.9), kind=kCustom, calls=%fused_computation.1 | custom fusion | bytes 212992 | tf_op jit(solution)/shard_map/jit(_take)/gather | solution.py:120
  137.4 7.5 %multiply_reduce_fusion = f32[6,1024]{0,1:T(8,128)S(1)} fusion(f32[6,1024,4]{0,2,1:T(4,128)} %bitcast.62, f32[1024,4]{1,0:T(8,128)S(1)} %copy.85, pred[1024,4]{1,0:T(8,128)(4,1)} %copy.79), kind=kLoop, calls=%fused_computation.22 | loop fusion | flops 67584 | bytes 143360 | tf_op jit(solution)/shard_map/reduce_sum | solution.py:121
  145.3 1.5 fusion.12
  146.8 2.0 copy.86
  148.9 2.5 fusion.24
  151.9 1.3 copy-done.1
  154.1 14.9 %scatter_custom_fusion.1 = f32[3,8192]{0,1:T(8,128)} fusion(s32[4096]{0:T(1024)} %bitcast.75, f32[3,4096]{0,1:T(8,128)S(1)} %bitcast.59, f32[]{:T(128)} %constant.32.clone.1, f32[4096]{0:T(1024)} %mul.202), kind=kCustom, calls=%fused_computation.18 | custom fusion | flops 12288 | bytes 164352 | tf_op jit(solution)/shard_map/scatter | solution.py:134
  169.0 3.5 %copy.90 = f32[3,32,256]{2,0,1:T(4,128)} copy(f32[3,32,256]{0,2,1:T(8,128)} %bitcast.57) | data formatting | bytes 196608 | tf_op jit(solution)/shard_map/all_to_all | solution.py:135
  172.4 9.8 %all-to-all-start.2 = ((f32[3,32,256]{2,0,1:T(4,128)}), f32[3,32,256]{2,0,1:T(4,128)S(1)}, u32[]{:S(2)}, u32[]{:S(2)}) async-start(f32[3,32,256]{2,0,1:T(4,128)} %copy.90), calls=%async_computation.2 | async-start | bytes 262144 | tf_op jit(solution)/shard_map/all_to_all | solution.py:135
  182.4 2.0 collective-permute-start.7
  184.4 1.3 collective-permute-start.6
  186.5 2.8 %all-to-all-done.2 = f32[3,32,256]{2,0,1:T(4,128)S(1)} async-done(((f32[3,32,256]{2,0,1:T(4,128)}), f32[3,32,256]{2,0,1:T(4,128)S(1)}, u32[]{:S(2)}, u32[]{:S(2)}) %all-to-all-start.2) | async-done | bytes 98336 | tf_op jit(solution)/shard_map/all_to_all | solution.py:135
  189.3 2.6 %copy.91 = f32[8192,3]{1,0:T(8,128)} copy(f32[8192,3]{0,1:T(4,128)S(1)} %bitcast.68) | data formatting | bytes 196608 | tf_op jit(solution)/shard_map/all_to_all | solution.py:135
  191.9 57.3 %scatter_custom_fusion.2 = f32[3,16384]{0,1:T(8,128)} fusion(s32[8192]{0:T(1024)} %bitcast.71, f32[8192,3]{1,0:T(8,128)} %copy.91, f32[]{:T(128)} %constant.32.clone.1), kind=kCustom, calls=%fused_computation.5 | custom fusion | flops 24576 | bytes 197120 | tf_op jit(solution)/shard_map/scatter-add | solution.py:139
  249.3 5.3 %copy.92 = f32[3,128,128]{2,1,0:T(8,128)S(1)} copy(f32[3,128,128]{0,2,1:T(8,128)} %bitcast.56) | data formatting | bytes 393216 | tf_op jit(solution)/shard_map/reshape | solution.py:140
  254.6 1.8 multiply_add_fusion
  (98 shorter events, 24.2 us)
Async XLA Ops:
  2.6 11.3 %copy-start.11 = (s32[1024,4]{0,1:T(4,128)S(1)}, s32[1024,4]{0,1:T(4,128)}, u32[]{:S(2)}) copy-start(s32[1024,4]{0,1:T(4,128)} %param.11) | copy-start | bytes 49156
  3.5 33.6 %copy-start = (f32[4,32,32,128]{3,2,1,0:T(8,128)S(1)}, f32[4,32,32,128]{3,2,1,0:T(8,128)}, u32[]{:S(2)}) copy-start(f32[4,32,32,128]{3,2,1,0:T(8,128)} %param.7) | copy-start | bytes 6291460
  12.7 32.0 %copy-start.4 = (f32[3,128,128]{2,1,0:T(8,128)S(1)}, f32[3,128,128]{2,1,0:T(8,128)}, u32[]{:S(2)}) copy-start(f32[3,128,128]{2,1,0:T(8,128)} %param.8) | copy-start | bytes 589828
  14.8 22.3 %copy-start.7 = (s32[4096]{0:T(1024)}, s32[4096]{0:T(1024)S(1)}, u32[]{:S(2)}) copy-start(s32[4096]{0:T(1024)S(1)} %fusion.21) | copy-start | bytes 49156
  14.9 37.2 %copy-start.10 = (s32[4096,1]{0,1:T(1,128)}, s32[4096,1]{0,1:T(1,128)S(1)}, u32[]{:S(2)}) copy-start(s32[4096,1]{0,1:T(1,128)S(1)} %compare_select_fusion.1) | copy-start | bytes 49156
  31.0 34.5 %all-to-all-start = ((s32[32,256,1]{1,2,0:T(1,128)}), s32[32,256,1]{1,2,0:T(1,128)}, u32[]{:S(2)}, u32[]{:S(2)}) async-start(s32[32,256,1]{1,2,0:T(1,128)} %bitcast.5), calls=%async_computation | async-start | bytes 65536 | tf_op jit(solution)/shard_map/all_to_all | solution.py:113
  37.9 19.1 %copy-start.5 = (f32[3,128,128]{2,1,0:T(8,128)S(1)}, f32[3,128,128]{2,1,0:T(8,128)}, u32[]{:S(2)}) copy-start(f32[3,128,128]{2,1,0:T(8,128)} %param.9) | copy-start | bytes 589828
  37.9 68.9 %collective-permute-start.1 = (f32[4,3,32,128]{3,2,1,0:T(8,128)}, f32[4,3,32,128]{3,2,1,0:T(8,128)}, u32[]{:S(2)}, u32[]{:S(2)}) collective-permute-start(f32[4,3,32,128]{3,2,1,0:T(8,128)} %get-tuple-element.34), channel_id=1, source_target_pairs={{0,4},{4,8},{8,12},{12,16},{16,20},{20,24},{24,28},{1,5},{5,9},{9,... | collective-permute-start | bytes 589832 | tf_op jit(solution)/shard_map/ppermute | solution.py:20
  41.4 67.3 %collective-permute-start = (f32[4,3,32,128]{3,2,1,0:T(8,128)}, f32[4,3,32,128]{3,2,1,0:T(8,128)}, u32[]{:S(2)}, u32[]{:S(2)}) collective-permute-start(f32[4,3,32,128]{3,2,1,0:T(8,128)} %get-tuple-element.33), channel_id=1, source_target_pairs={{4,0},{8,4},{12,8},{16,12},{20,16},{24,20},{28,24},{5,1},{9,5},{13... | collective-permute-start | bytes 589832 | tf_op jit(solution)/shard_map/ppermute | solution.py:21
  45.3 19.4 %collective-permute-start.4 = (f32[3,1,128]{2,1,0:T(1,128)}, f32[3,1,128]{2,1,0:T(1,128)S(1)}, u32[]{:S(2)}, u32[]{:S(2)}) collective-permute-start(f32[3,1,128]{2,1,0:T(1,128)} %get-tuple-element.38), channel_id=1, source_target_pairs={{4,0},{8,4},{12,8},{16,12},{20,16},{24,20},{28,24},{5,1},{9,5},{13... | collective-permute-start | bytes 4616 | tf_op jit(solution)/shard_map/ppermute | solution.py:21
  48.4 16.3 %collective-permute-start.5 = (f32[3,1,128]{2,1,0:T(1,128)}, f32[3,1,128]{2,1,0:T(1,128)}, u32[]{:S(2)}, u32[]{:S(2)}) collective-permute-start(f32[3,1,128]{2,1,0:T(1,128)} %get-tuple-element.37), channel_id=1, source_target_pairs={{0,4},{4,8},{8,12},{12,16},{16,20},{20,24},{24,28},{1,5},{5,9},{9,... | collective-permute-start | bytes 4616 | tf_op jit(solution)/shard_map/ppermute | solution.py:20
  52.1 9.6 %copy-start.14 = (s32[128]{0:T(128)}, s32[128]{0:T(128)S(1)}, u32[]{:S(2)}) copy-start(s32[128]{0:T(128)S(1)} %iota_add_fusion.1) | copy-start | bytes 1540
  52.1 9.6 %copy-start.16 = (pred[128]{0:T(512)(128)(4,1)}, pred[128]{0:T(512)(128)(4,1)S(1)}, u32[]{:S(2)}) copy-start(pred[128]{0:T(512)(128)(4,1)S(1)} %iota_compare_fusion.2) | copy-start | bytes 388
  57.0 4.7 %copy-start.12 = (f32[1024,4]{0,1:T(4,128)S(1)}, f32[1024,4]{0,1:T(4,128)}, u32[]{:S(2)}) copy-start(f32[1024,4]{0,1:T(4,128)} %param.12) | copy-start | bytes 49156
  66.2 31.3 %copy-start.8 = (s32[8192,1]{0,1:T(1,128)}, s32[8192,1]{0,1:T(1,128)S(1)}, u32[]{:S(2)}) copy-start(s32[8192,1]{0,1:T(1,128)S(1)} %compare_select_fusion) | copy-start | bytes 98308
  101.9 16.5 %all-to-all-start.1 = ((f32[6,32,256]{2,0,1:T(8,128)}), f32[6,32,256]{2,0,1:T(8,128)S(1)}, u32[]{:S(2)}, u32[]{:S(2)}) async-start(f32[6,32,256]{2,0,1:T(8,128)} %broadcast_select_fusion), calls=%async_computation.1 | async-start | bytes 524288 | tf_op jit(solution)/shard_map/all_to_all | solution.py:119
  109.7 6.4 %collective-permute-start.3 = (f32[4,38,3,128]{3,2,1,0:T(4,128)S(1)}, f32[4,38,3,128]{3,2,1,0:T(4,128)S(1)}, u32[]{:S(2)}, u32[]{:S(2)}) collective-permute-start(f32[4,38,3,128]{3,2,1,0:T(4,128)S(1)} %get-tuple-element.25), channel_id=1, source_target_pairs={{1,0},{2,1},{3,2},{5,4},{6,5},{7,6},{9,8},{10,9},{11,10},{13,12},{... | collective-permute-start | bytes 700424 | tf_op jit(solution)/shard_map/ppermute | solution.py:21
  111.0 5.1 %collective-permute-start.2 = (f32[4,38,3,128]{3,2,1,0:T(4,128)S(1)}, f32[4,38,3,128]{3,2,1,0:T(4,128)S(1)}, u32[]{:S(2)}, u32[]{:S(2)}) collective-permute-start(f32[4,38,3,128]{3,2,1,0:T(4,128)S(1)} %get-tuple-element.24), channel_id=1, source_target_pairs={{0,1},{1,2},{2,3},{4,5},{5,6},{6,7},{8,9},{9,10},{10,11},{12,13},{... | collective-permute-start | bytes 700424 | tf_op jit(solution)/shard_map/ppermute | solution.py:20
  118.3 2.6 %copy-start.9 = (s32[4096]{0:T(1024)S(1)}, s32[4096]{0:T(1024)}, u32[]{:S(2)}) copy-start(s32[4096]{0:T(1024)} %broadcast_clamp_fusion.1) | copy-start | bytes 49156
  137.3 7.9 %copy-start.3 = (f32[1,32,32,128]{3,2,1,0:T(8,128)S(1)}, f32[1,32,32,128]{3,2,1,0:T(8,128)}, u32[]{:S(2)}) copy-start(f32[1,32,32,128]{3,2,1,0:T(8,128)} %get-tuple-element.28) | copy-start | bytes 1572868
  137.3 7.9 %copy-start.15 = (s32[128]{0:T(128)S(1)}, s32[128]{0:T(128)}, u32[]{:S(2)}) copy-start(s32[128]{0:T(128)} %copy-done.14) | copy-start | bytes 1540
  137.4 7.9 %copy-start.17 = (pred[128]{0:T(512)(128)(4,1)S(1)}, pred[128]{0:T(512)(128)(4,1)}, u32[]{:S(2)}) copy-start(pred[128]{0:T(512)(128)(4,1)} %copy-done.16) | copy-start | bytes 388
  137.4 8.0 %copy-start.18 = (f32[128]{0:T(128)S(1)}, f32[128]{0:T(128)}, u32[]{:S(2)}) copy-start(f32[128]{0:T(128)} %broadcast_multiply_fusion.2) | copy-start | bytes 1540
  144.9 4.0 %copy-start.2 = (f32[1024,128]{1,0:T(8,128)S(1)}, f32[1024,128]{1,0:T(8,128)}, u32[]{:S(2)}) copy-start(f32[1024,128]{1,0:T(8,128)} %copy.87) | copy-start | bytes 1572868
  151.4 2.1 copy-start.13
  151.9 1.3 copy-start.1
  172.4 16.9 %all-to-all-start.2 = ((f32[3,32,256]{2,0,1:T(4,128)}), f32[3,32,256]{2,0,1:T(4,128)S(1)}, u32[]{:S(2)}, u32[]{:S(2)}) async-start(f32[3,32,256]{2,0,1:T(4,128)} %copy.90), calls=%async_computation.2 | async-start | bytes 262144 | tf_op jit(solution)/shard_map/all_to_all | solution.py:135
  182.4 72.2 %collective-permute-start.7 = (f32[3,130,1]{2,1,0:T(8,128)S(1)}, f32[3,130,1]{2,1,0:T(8,128)S(1)}, u32[]{:S(2)}, u32[]{:S(2)}) collective-permute-start(f32[3,130,1]{2,1,0:T(8,128)S(1)} %get-tuple-element.36), channel_id=1, source_target_pairs={{0,1},{1,2},{2,3},{4,5},{5,6},{6,7},{8,9},{9,10},{10,11},{12,13},{... | collective-permute-start | bytes 4688 | tf_op jit(solution)/shard_map/ppermute | solution.py:20
  184.4 70.2 %collective-permute-start.6 = (f32[3,130,1]{2,1,0:T(8,128)S(1)}, f32[3,130,1]{2,1,0:T(8,128)S(1)}, u32[]{:S(2)}, u32[]{:S(2)}) collective-permute-start(f32[3,130,1]{2,1,0:T(8,128)S(1)} %get-tuple-element.35), channel_id=1, source_target_pairs={{1,0},{2,1},{3,2},{5,4},{6,5},{7,6},{9,8},{10,9},{11,10},{13,12},{... | collective-permute-start | bytes 4688 | tf_op jit(solution)/shard_map/ppermute | solution.py:21
  249.3 5.3 %copy-start.6 = (f32[3,128,128]{2,1,0:T(8,128)S(1)}, f32[3,128,128]{2,1,0:T(8,128)}, u32[]{:S(2)}) copy-start(f32[3,128,128]{2,1,0:T(8,128)} %param.9) | copy-start | bytes 589828
where the time goes:
time: 258 us; the launch traced here: 256 us
  other arithmetic  104 us (40%)
  local copies, waits for them, and re-layouts  104 us (40%)
  starting transfers between devices  41.3 us (16%)
  waiting for transfers between devices  2.85 us (1%)
    scatter-add x1, other arithmetic, body(): shell_force = jnp.zeros((3, rows_x * rows_y), jnp.float32).at[:, asked_no...  57.3 us
    gather x2, local copies, waits for them, and re-layouts, body(): picked = jnp.take(stacked, asked_nodes, axis=1)  34.1 us
    gather x1, local copies, waits for them, and re-layouts, body(): motion = jnp.take(replies, slot_index, axis=1).reshape(6, points, stencil)  16.4 us
    scatter x1, local copies, waits for them, and re-layouts, body(): jnp.zeros((devices * capacity,), jnp.int32).at[slot_index].set(node_ids)  16.1 us
    scatter x1, other arithmetic, body(): jnp.zeros((3, devices * capacity), jnp.float32).at[:, slot_index]  14.9 us
    ppermute x4, starting transfers between devices, with_halo(): before = lax.ppermute(last, axis, up)  11.5 us
    all_to_all x1, starting transfers between devices, body(): lax.all_to_all(outgoing, ('span', 'chord'), split_axis=1, concat_axis=1,...  9.79 us
    another operation x3, other arithmetic  9.62 us
  transfers between devices with their start and end apart: 11, of which 1 were waited for; matrix products, arithmetic and copies ran while one was open for 49% of the time, Pallas kernels for 0%

commit v1 on v0

--- a/solution.py
+++ b/solution.py
@@ -2,6 +2,7 @@
 import jax.numpy as jnp
 from jax import lax
 from jax.sharding import PartitionSpec as P
+from jax.lax import all_to_all, axis_size
 
 flow_speed = 0.5
 time_step = 0.4
@@ -132,7 +133,15 @@
     surface_load = normals * pressure[None]
     contrib = (surface_load[:, :, None] * rbf_weight[None]).reshape(3, -1)
     outgoing = jnp.zeros((3, devices * capacity), jnp.float32).at[:, slot_index].set(contrib)
-    arrived = lax.all_to_all(outgoing, ("span", "chord"), split_axis=1, concat_axis=1, tiled=True)
+    arrived = jnp.concatenate(
+        all_to_all(
+            jnp.stack(jnp.split(outgoing, axis_size(("span", "chord")), axis=1), axis=0),
+            concat_axis=0,
+            axis_name=("span", "chord"),
+            split_axis=0,
+        ),
+        axis=1,
+    )
     shell_force = (
         jnp.zeros((3, rows_x * rows_y), jnp.float32)
         .at[:, asked_nodes]

time: 258 us -> 315 us (1.22)
  local copies, waits for them, and re-layouts: 104 us -> 157 us
    unnamed x44 -> x63, local copies, waits for them, and re-layouts: 5.4 us -> 55.3 us
    all_to_all x2 -> x0, local copies, waits for them, and re-layouts: 6.09 us -> none  [body(): lax.all_to_all(outgoing, ('span', 'chord'), split_axis=1, concat_axis=1,...]
    another operation x0 -> x2, local copies, waits for them, and re-layouts: none -> 5.06 us  [body(): jnp.stack(jnp.split(outgoing, axis_size(('span', 'chord')), axis=1), axis=0)]
  transfers between devices with their start and end apart: 11 -> 11, of which waited for: 1 -> 1; matrix products, arithmetic and copies ran while one was open for 49% -> 40% of each run, Pallas kernels for 0% -> 0%
where the time goes in v1:
time: 315 us; the launch traced here: 313 us
  local copies, waits for them, and re-layouts  157 us (50%)
  other arithmetic  107 us (34%)
  starting transfers between devices  41.4 us (13%)
  matrix products  3.27 us (1%)
    scatter-add x1, other arithmetic, body(): shell_force = jnp.zeros((3, rows_x * rows_y), jnp.float32).at[:, asked_no...  57.3 us
    unnamed x63, local copies, waits for them, and re-layouts  55.3 us
    gather x2, local copies, waits for them, and re-layouts, body(): picked = jnp.take(stacked, asked_nodes, axis=1)  34.1 us
    gather x1, local copies, waits for them, and re-layouts, body(): motion = jnp.take(replies, slot_index, axis=1).reshape(6, points, stencil)  16.4 us
    scatter x1, local copies, waits for them, and re-layouts, body(): jnp.zeros((devices * capacity,), jnp.int32).at[slot_index].set(node_ids)  16.3 us
    scatter x1, other arithmetic, body(): jnp.zeros((3, devices * capacity), jnp.float32).at[:, slot_index]  14.9 us
    ppermute x4, starting transfers between devices, with_halo(): before = lax.ppermute(last, axis, up)  11.3 us
    another operation x3, other arithmetic  10.9 us
  transfers between devices with their start and end apart: 11, of which 1 were waited for; matrix products, arithmetic and copies ran while one was open for 40% of the time, Pallas kernels for 0%

profile of v1, /device:TPU:8, one launch (start us, length us, event | category | flops | bytes accessed | tf_op | source)
XLA Modules:
  0.0 312.8 jit_solution(16413506040312418387)
XLA Ops:
  4.9 9.2 %reduce-window.6 = s32[32,32,128]{2,1,0:T(8,128)S(1)} reduce-window(s32[32,32,128]{2,1,0:T(8,128)S(1)} %fusion.25, s32[]{:T(128)} %constant.34.clone.1), window={size=1x1x128 pad=0_0x0_0x127_0}, to_apply=%region_0.0 | reduce-window | flops 16646144 | bytes 1048580 | tf_op jit(solution)/shard_map/reduce-window
  20.9 16.3 %scatter_custom_fusion = s32[8192]{0:T(1024)} fusion(s32[4096]{0:T(1024)S(1)} %bitcast.201, s32[4096]{0:T(1024)} %reshape.179, s32[]{:T(128)} %constant.34.clone.1), kind=kCustom, calls=%fused_computation.188 | custom fusion | bytes 33280 | tf_op jit(solution)/shard_map/scatter | solution.py:113
  37.2 6.1 %all-to-all-start = ((s32[32,256,1]{1,2,0:T(1,128)}), s32[32,256,1]{1,2,0:T(1,128)}, u32[]{:S(2)}, u32[]{:S(2)}) async-start(s32[32,256,1]{1,2,0:T(1,128)} %bitcast.5), calls=%async_computation | async-start | bytes 65536 | tf_op jit(solution)/shard_map/all_to_all | solution.py:114
  44.1 3.4 %collective-permute-start.1 = (f32[4,3,32,128]{3,2,1,0:T(8,128)}, f32[4,3,32,128]{3,2,1,0:T(8,128)}, u32[]{:S(2)}, u32[]{:S(2)}) collective-permute-start(f32[4,3,32,128]{3,2,1,0:T(8,128)} %get-tuple-element.34), channel_id=1, source_target_pairs={{0,4},{4,8},{8,12},{12,16},{16,20},{20,24},{24,28},{1,5},{5,9},{9,... | collective-permute-start | bytes 589832 | tf_op jit(solution)/shard_map/ppermute | solution.py:21
  47.5 3.4 %collective-permute-start = (f32[4,3,32,128]{3,2,1,0:T(8,128)}, f32[4,3,32,128]{3,2,1,0:T(8,128)}, u32[]{:S(2)}, u32[]{:S(2)}) collective-permute-start(f32[4,3,32,128]{3,2,1,0:T(8,128)} %get-tuple-element.33), channel_id=1, source_target_pairs={{4,0},{8,4},{12,8},{16,12},{20,16},{24,20},{28,24},{5,1},{9,5},{13... | collective-permute-start | bytes 589832 | tf_op jit(solution)/shard_map/ppermute | solution.py:22
  51.4 3.1 collective-permute-start.4
  54.6 2.7 collective-permute-start.5
  63.1 4.7 %copy.146 = f32[6,128,128]{0,2,1:T(8,128)} copy(f32[6,128,128]{2,1,0:T(8,128)S(1)} %pad_maximum_fusion.1) | data formatting | bytes 786432 | tf_op jit(solution)/shard_map/concatenate | solution.py:118
  72.3 31.2 %gather_fusion = f32[8192,6]{1,0:T(8,128)} fusion(f32[6,16384]{0,1:T(8,128)} %bitcast.186, s32[8192]{0:T(1024)S(1)} %broadcast_clamp_fusion), kind=kCustom, calls=%fused_computation | custom fusion | bytes 425984 | tf_op jit(solution)/shard_map/jit(_take)/gather | solution.py:119
  103.6 2.8 copy.147
  108.0 4.9 %all-to-all-start.1 = ((f32[6,32,256]{2,0,1:T(8,128)}), f32[6,32,256]{2,0,1:T(8,128)S(1)}, u32[]{:S(2)}, u32[]{:S(2)}) async-start(f32[6,32,256]{2,0,1:T(8,128)} %broadcast_select_fusion), calls=%async_computation.1 | async-start | bytes 524288 | tf_op jit(solution)/shard_map/all_to_all | solution.py:120
  117.1 3.2 %collective-permute-start.2 = (f32[4,38,3,128]{3,2,1,0:T(4,128)S(1)}, f32[4,38,3,128]{3,2,1,0:T(4,128)S(1)}, u32[]{:S(2)}, u32[]{:S(2)}) collective-permute-start(f32[4,38,3,128]{3,2,1,0:T(4,128)S(1)} %get-tuple-element.24), channel_id=1, source_target_pairs={{0,1},{1,2},{2,3},{4,5},{5,6},{6,7},{8,9},{9,10},{10,11},{12,13},{... | collective-permute-start | bytes 700424 | tf_op jit(solution)/shard_map/ppermute | solution.py:21
  120.4 1.9 fusion.3
  122.8 1.6 fusion.14
  124.5 2.6 copy.148
  127.1 16.4 %gather_fusion.1 = f32[4096,6]{1,0:T(8,128)} fusion(f32[6,8192]{0,1:T(8,128)} %bitcast.188, s32[4096]{0:T(1024)S(1)} %copy-done.7), kind=kCustom, calls=%fused_computation.1 | custom fusion | bytes 212992 | tf_op jit(solution)/shard_map/jit(_take)/gather | solution.py:121
  143.5 7.5 %multiply_reduce_fusion = f32[6,1024]{0,1:T(8,128)S(1)} fusion(f32[6,1024,4]{0,2,1:T(4,128)} %bitcast.190, f32[1024,4]{1,0:T(8,128)S(1)} %copy.149, pred[1024,4]{1,0:T(8,128)(4,1)} %copy.143), kind=kLoop, calls=%fused_computation.22 | loop fusion | flops 67584 | bytes 143360 | tf_op jit(solution)/shard_map/reduce_sum | solution.py:122
  151.3 2.6 fusion.12
  155.1 2.5 fusion.24
  160.4 14.9 %scatter_custom_fusion.1 = f32[3,8192]{0,1:T(8,128)} fusion(s32[4096]{0:T(1024)} %bitcast.203, f32[3,4096]{0,1:T(8,128)S(1)} %bitcast.187, f32[]{:T(128)} %constant.32.clone.1, f32[4096]{0:T(1024)} %mul.202), kind=kCustom, calls=%fused_computation.18 | custom fusion | flops 12288 | bytes 164352 | tf_op jit(solution)/shard_map/scatter | solution.py:135
  189.4 1.6 fusion.57
  190.9 1.6 fusion.56
  222.3 1.6 fusion.36
  223.9 1.6 fusion.35
  225.5 3.5 %copy.154 = f32[32,3,256]{2,1,0:T(4,128)} copy(f32[32,3,256]{1,2,0:T(8,128)} %fusion.35) | data formatting | bytes 196608 | tf_op jit(solution)/shard_map/stack | solution.py:138
  228.9 9.8 %all-to-all-start.2 = ((f32[32,3,256]{2,1,0:T(4,128)}), f32[32,3,256]{2,1,0:T(4,128)S(1)}, u32[]{:S(2)}, u32[]{:S(2)}) async-start(f32[32,3,256]{2,1,0:T(4,128)} %copy.154), calls=%async_computation.2 | async-start | bytes 262144 | tf_op jit(solution)/shard_map/all_to_all | solution.py:137
  238.9 2.0 collective-permute-start.7
  243.2 2.6 all-to-all-done.2
  245.8 2.6 copy.155
  248.5 57.3 %scatter_custom_fusion.2 = f32[3,16384]{0,1:T(8,128)} fusion(s32[8192]{0:T(1024)} %bitcast.199, f32[8192,3]{1,0:T(8,128)} %copy.155, f32[]{:T(128)} %constant.32.clone.1), kind=kCustom, calls=%fused_computation.5 | custom fusion | flops 24576 | bytes 197120 | tf_op jit(solution)/shard_map/scatter-add | solution.py:148
  305.8 5.3 %copy.156 = f32[3,128,128]{2,1,0:T(8,128)S(1)} copy(f32[3,128,128]{0,2,1:T(8,128)} %bitcast.185) | data formatting | bytes 393216 | tf_op jit(solution)/shard_map/reshape | solution.py:149
  311.1 1.7 multiply_add_fusion
  (118 shorter events, 79.5 us)
Async XLA Ops:
  0.6 42.7 %copy-start = (f32[4,32,32,128]{3,2,1,0:T(8,128)S(1)}, f32[4,32,32,128]{3,2,1,0:T(8,128)}, u32[]{:S(2)}) copy-start(f32[4,32,32,128]{3,2,1,0:T(8,128)} %param.7) | copy-start | bytes 6291460
  1.5 49.3 %copy-start.2 = (f32[3,128,128]{2,1,0:T(8,128)S(1)}, f32[3,128,128]{2,1,0:T(8,128)}, u32[]{:S(2)}) copy-start(f32[3,128,128]{2,1,0:T(8,128)} %param.8) | copy-start | bytes 589828
  14.1 49.0 %copy-start.3 = (f32[3,128,128]{2,1,0:T(8,128)S(1)}, f32[3,128,128]{2,1,0:T(8,128)}, u32[]{:S(2)}) copy-start(f32[3,128,128]{2,1,0:T(8,128)} %param.9) | copy-start | bytes 589828
  19.6 0.6 copy-start.5
  20.9 37.3 %copy-start.8 = (s32[4096,1]{0,1:T(1,128)}, s32[4096,1]{0,1:T(1,128)S(1)}, u32[]{:S(2)}) copy-start(s32[4096,1]{0,1:T(1,128)S(1)} %compare_select_fusion.1) | copy-start | bytes 49156
  37.2 34.3 %all-to-all-start = ((s32[32,256,1]{1,2,0:T(1,128)}), s32[32,256,1]{1,2,0:T(1,128)}, u32[]{:S(2)}, u32[]{:S(2)}) async-start(s32[32,256,1]{1,2,0:T(1,128)} %bitcast.5), calls=%async_computation | async-start | bytes 65536 | tf_op jit(solution)/shard_map/all_to_all | solution.py:114
  44.1 68.8 %collective-permute-start.1 = (f32[4,3,32,128]{3,2,1,0:T(8,128)}, f32[4,3,32,128]{3,2,1,0:T(8,128)}, u32[]{:S(2)}, u32[]{:S(2)}) collective-permute-start(f32[4,3,32,128]{3,2,1,0:T(8,128)} %get-tuple-element.34), channel_id=1, source_target_pairs={{0,4},{4,8},{8,12},{12,16},{16,20},{20,24},{24,28},{1,5},{5,9},{9,... | collective-permute-start | bytes 589832 | tf_op jit(solution)/shard_map/ppermute | solution.py:21
  47.5 67.3 %collective-permute-start = (f32[4,3,32,128]{3,2,1,0:T(8,128)}, f32[4,3,32,128]{3,2,1,0:T(8,128)}, u32[]{:S(2)}, u32[]{:S(2)}) collective-permute-start(f32[4,3,32,128]{3,2,1,0:T(8,128)} %get-tuple-element.33), channel_id=1, source_target_pairs={{4,0},{8,4},{12,8},{16,12},{20,16},{24,20},{28,24},{5,1},{9,5},{13... | collective-permute-start | bytes 589832 | tf_op jit(solution)/shard_map/ppermute | solution.py:22
  51.4 19.4 %collective-permute-start.4 = (f32[3,1,128]{2,1,0:T(1,128)}, f32[3,1,128]{2,1,0:T(1,128)S(1)}, u32[]{:S(2)}, u32[]{:S(2)}) collective-permute-start(f32[3,1,128]{2,1,0:T(1,128)} %get-tuple-element.38), channel_id=1, source_target_pairs={{4,0},{8,4},{12,8},{16,12},{20,16},{24,20},{28,24},{5,1},{9,5},{13... | collective-permute-start | bytes 4616 | tf_op jit(solution)/shard_map/ppermute | solution.py:22
  54.6 16.3 %collective-permute-start.5 = (f32[3,1,128]{2,1,0:T(1,128)}, f32[3,1,128]{2,1,0:T(1,128)}, u32[]{:S(2)}, u32[]{:S(2)}) collective-permute-start(f32[3,1,128]{2,1,0:T(1,128)} %get-tuple-element.37), channel_id=1, source_target_pairs={{0,4},{4,8},{8,12},{12,16},{16,20},{20,24},{24,28},{1,5},{5,9},{9,... | collective-permute-start | bytes 4616 | tf_op jit(solution)/shard_map/ppermute | solution.py:21
  58.2 9.7 %copy-start.11 = (s32[128]{0:T(128)}, s32[128]{0:T(128)S(1)}, u32[]{:S(2)}) copy-start(s32[128]{0:T(128)S(1)} %iota_add_fusion.1) | copy-start | bytes 1540
  58.2 9.7 %copy-start.12 = (pred[128]{0:T(512)(128)(4,1)}, pred[128]{0:T(512)(128)(4,1)S(1)}, u32[]{:S(2)}) copy-start(pred[128]{0:T(512)(128)(4,1)S(1)} %iota_compare_fusion.2) | copy-start | bytes 388
  63.1 4.7 %copy-start.9 = (f32[1024,4]{0,1:T(4,128)S(1)}, f32[1024,4]{0,1:T(4,128)}, u32[]{:S(2)}) copy-start(f32[1024,4]{0,1:T(4,128)} %param.12) | copy-start | bytes 49156
  72.3 31.3 %copy-start.6 = (s32[8192,1]{0,1:T(1,128)}, s32[8192,1]{0,1:T(1,128)S(1)}, u32[]{:S(2)}) copy-start(s32[8192,1]{0,1:T(1,128)S(1)} %compare_select_fusion) | copy-start | bytes 98308
  108.0 16.5 %all-to-all-start.1 = ((f32[6,32,256]{2,0,1:T(8,128)}), f32[6,32,256]{2,0,1:T(8,128)S(1)}, u32[]{:S(2)}, u32[]{:S(2)}) async-start(f32[6,32,256]{2,0,1:T(8,128)} %broadcast_select_fusion), calls=%async_computation.1 | async-start | bytes 524288 | tf_op jit(solution)/shard_map/all_to_all | solution.py:120
  115.8 6.4 %collective-permute-start.3 = (f32[4,38,3,128]{3,2,1,0:T(4,128)S(1)}, f32[4,38,3,128]{3,2,1,0:T(4,128)S(1)}, u32[]{:S(2)}, u32[]{:S(2)}) collective-permute-start(f32[4,38,3,128]{3,2,1,0:T(4,128)S(1)} %get-tuple-element.25), channel_id=1, source_target_pairs={{1,0},{2,1},{3,2},{5,4},{6,5},{7,6},{9,8},{10,9},{11,10},{13,12},{... | collective-permute-start | bytes 700424 | tf_op jit(solution)/shard_map/ppermute | solution.py:22
  117.1 5.1 %collective-permute-start.2 = (f32[4,38,3,128]{3,2,1,0:T(4,128)S(1)}, f32[4,38,3,128]{3,2,1,0:T(4,128)S(1)}, u32[]{:S(2)}, u32[]{:S(2)}) collective-permute-start(f32[4,38,3,128]{3,2,1,0:T(4,128)S(1)} %get-tuple-element.24), channel_id=1, source_target_pairs={{0,1},{1,2},{2,3},{4,5},{5,6},{6,7},{8,9},{9,10},{10,11},{12,13},{... | collective-permute-start | bytes 700424 | tf_op jit(solution)/shard_map/ppermute | solution.py:21
  122.8 4.3 %copy-start.7 = (s32[4096]{0:T(1024)S(1)}, s32[4096]{0:T(1024)}, u32[]{:S(2)}) copy-start(s32[4096]{0:T(1024)} %broadcast_clamp_fusion.1) | copy-start | bytes 49156
  157.6 2.1 copy-start.10
  158.1 1.3 copy-start.1
  228.9 16.9 %all-to-all-start.2 = ((f32[32,3,256]{2,1,0:T(4,128)}), f32[32,3,256]{2,1,0:T(4,128)S(1)}, u32[]{:S(2)}, u32[]{:S(2)}) async-start(f32[32,3,256]{2,1,0:T(4,128)} %copy.154), calls=%async_computation.2 | async-start | bytes 262144 | tf_op jit(solution)/shard_map/all_to_all | solution.py:137
  238.9 72.2 %collective-permute-start.7 = (f32[3,130,1]{2,1,0:T(8,128)S(1)}, f32[3,130,1]{2,1,0:T(8,128)S(1)}, u32[]{:S(2)}, u32[]{:S(2)}) collective-permute-start(f32[3,130,1]{2,1,0:T(8,128)S(1)} %get-tuple-element.36), channel_id=1, source_target_pairs={{0,1},{1,2},{2,3},{4,5},{5,6},{6,7},{8,9},{9,10},{10,11},{12,13},{... | collective-permute-start | bytes 4688 | tf_op jit(solution)/shard_map/ppermute | solution.py:21
  240.9 70.2 %collective-permute-start.6 = (f32[3,130,1]{2,1,0:T(8,128)S(1)}, f32[3,130,1]{2,1,0:T(8,128)S(1)}, u32[]{:S(2)}, u32[]{:S(2)}) collective-permute-start(f32[3,130,1]{2,1,0:T(8,128)S(1)} %get-tuple-element.35), channel_id=1, source_target_pairs={{1,0},{2,1},{3,2},{5,4},{6,5},{7,6},{9,8},{10,9},{11,10},{13,12},{... | collective-permute-start | bytes 4688 | tf_op jit(solution)/shard_map/ppermute | solution.py:22
  305.8 5.3 %copy-start.4 = (f32[3,128,128]{2,1,0:T(8,128)S(1)}, f32[3,128,128]{2,1,0:T(8,128)}, u32[]{:S(2)}) copy-start(f32[3,128,128]{2,1,0:T(8,128)} %param.9) | copy-start | bytes 589828
